TPU v7x, 128 devices: a whole 4x4x4 slice. The times are simulated.
128 devices in a mesh: front: 4 (over x_lo, core), row: 4 (over z), col: 8 (over y, x_hi).
Axes of the slice: x: 4 (x_hi: 2, x_lo: 2; x = x_hi * 2 + x_lo), y: 4, z: 4, core: 2. Of those that a mesh axis runs over, the one named last changes fastest.
Arguments:
- front_entries: float32 [4, 8192, 8192], P('front', 'row', 'col'), may hold values from -12 to 128, as said below
- kid_u: bfloat16 [16, 4096, 128], P('front', ('row', 'col')), may hold values from -0.7109375 to 0.7109375
- kid_v: bfloat16 [16, 4096, 128], P('front', ('row', 'col')), may hold values from -0.7109375 to 0.7109375
- kid_d: bfloat16 [16, 4096, 256], P('front', ('row', 'col')), may hold values from -2.09375 to 2.09375
- kid_counts: int32 [16], replicated, may hold values from 32 to 128
- kid_blocks: int32 [16, 16], replicated, may hold values from 0 to 31, as said below
Outputs:
- front_out: float32 [4, 8192, 8192], P('front', 'row', 'col')
Inputs may be any that keep to these rules, and one draw needn't show every extreme that they name: `front_entries`: diagonal entries lie between 64 and 128; the other entries are of order one. `kid_blocks`: each row holds distinct block positions in increasing order. `kid_counts`: rank columns at or beyond a child's count are padding.
All inputs are finite; a program needn't handle non-finite values.
Results may differ from a plain program's by a relative error of at most 0.004.
Values may be sent and summed in bfloat16 or wider, within the bound.
No kernel may reach another device: no remote copies, remote signals or barrier semaphores. Data moves between devices by JAX's collectives and lax.ppermute only.
A program may use at most 128 MiB of HBM per device.

v0:
```python
import jax
import jax.numpy as jnp
from jax import lax
from jax.sharding import Mesh
from jax.sharding import PartitionSpec as P

PANEL = 256
PANELS = 4
COL = ("col_0", "col_1")
ROW_COL = ("row", "col_0", "col_1")


def shifted(value, axis, by):
    peers = lax.axis_size(axis)
    return lax.ppermute(value, axis, [(i, (i + by) % peers) for i in range(peers)])


def from_root(value, axis, root):
    return lax.dynamic_index_in_dim(lax.all_gather(value, axis), root, 0, keepdims=False)


def broadcast_by_axis(value, axes, root):
    value = jnp.where(lax.axis_index(axes) == root, value, jnp.zeros_like(value))
    for axis in axes:
        value = lax.psum(value, axis)
    return value


def invert(block):
    gram = jnp.dot(block.T, block, precision=lax.Precision.HIGHEST)
    factor = jnp.linalg.cholesky(gram)
    return jax.scipy.linalg.cho_solve((factor, True), block.T)


def make_collector(blocks, row_offset, col_offset, row_width, col_width, rank_width, leaf_width):
    children = blocks.shape[0]
    block_count = blocks.shape[1]

    def place_rows(carry, piece, start):
        rows_u, cols_v, rows_d = carry
        length = piece.shape[1]
        child_rows = jnp.arange(length, dtype=jnp.int32)
        which_block = child_rows // leaf_width
        within = child_rows % leaf_width
        onehot = (which_block[:, None] == jnp.arange(block_count, dtype=jnp.int32)[None, :]).astype(
            jnp.int32
        )
        target = (
            jnp.sum(blocks[:, None, :] * onehot[None, :, :], axis=2) * leaf_width + within[None, :]
        )
        local_row = target - row_offset
        local_row = jnp.where((local_row >= 0) & (local_row < row_width), local_row, row_width)
        local_col = target - col_offset
        local_col = jnp.where((local_col >= 0) & (local_col < col_width), local_col, col_width)
        child_index = jnp.broadcast_to(jnp.arange(children, dtype=jnp.int32)[:, None], target.shape)
        rows_u = rows_u.at[local_row, child_index].set(piece[:, :, :rank_width], mode="drop")
        cols_v = cols_v.at[local_col, child_index].set(
            piece[:, :, rank_width : 2 * rank_width], mode="drop"
        )
        rows_d = rows_d.at[local_row].add(
            piece[:, :, 2 * rank_width :].astype(jnp.float32), mode="drop"
        )
        return (rows_u, cols_v, rows_d)

    empty_carry = (
        jnp.zeros((row_width, children, rank_width), jnp.bfloat16),
        jnp.zeros((col_width, children, rank_width), jnp.bfloat16),
        jnp.zeros((row_width, leaf_width), jnp.float32),
    )
    return (place_rows, empty_carry)


def expand_tile(collected, counts, row_offset, col_offset, leaf_width):
    rows_u, cols_v, rows_d = collected
    row_width, children, rank_width = rows_u.shape
    col_width = cols_v.shape[0]
    rank_mask = (jnp.arange(rank_width, dtype=jnp.int32)[None, :] < counts[:, None]).astype(
        jnp.bfloat16
    )
    masked_u = (rows_u * rank_mask[None, :, :]).reshape(row_width, children * rank_width)
    lowrank = lax.dot_general(
        masked_u,
        cols_v.reshape(col_width, children * rank_width),
        (((1,), (1,)), ((), ())),
        preferred_element_type=jnp.float32,
    )
    row_leaves = row_width // leaf_width
    col_leaves = col_width // leaf_width
    row_blocks = row_offset // leaf_width + jnp.arange(row_leaves, dtype=jnp.int32)
    col_blocks = col_offset // leaf_width + jnp.arange(col_leaves, dtype=jnp.int32)
    same_block = (row_blocks[:, None] == col_blocks[None, :]).astype(jnp.float32)
    stacked_d = rows_d.reshape(row_leaves, leaf_width, leaf_width)
    diagonal_part = (stacked_d[:, :, None, :] * same_block[:, None, :, None]).reshape(
        row_width, col_width
    )
    return lowrank + diagonal_part


def local(front_entries, kid_u, kid_v, kid_d, kid_counts, kid_blocks):
    children = kid_u.shape[0]
    rank_width = kid_u.shape[2]
    leaf_width = kid_d.shape[2]
    row_width = front_entries.shape[1]
    col_width = front_entries.shape[2]
    row_offset = lax.axis_index("row") * row_width
    col_offset = lax.axis_index(COL) * col_width
    front_count = lax.axis_size("front")
    packed = jnp.concatenate((kid_u, kid_v, kid_d), axis=2)
    moved = shifted(packed, "front", 1)
    first_child = (lax.axis_index("front") + front_count - 1) % front_count * children
    counts = lax.dynamic_slice_in_dim(kid_counts, first_child, children, 0)
    blocks = lax.dynamic_slice_in_dim(kid_blocks, first_child, children, 0)
    place_rows, empty_carry = make_collector(
        blocks, row_offset, col_offset, row_width, col_width, rank_width, leaf_width
    )
    collected = place_rows(
        empty_carry, lax.all_gather(moved, ROW_COL, axis=1, tiled=True), jnp.int32(0)
    )
    front = front_entries[0] + expand_tile(collected, counts, row_offset, col_offset, leaf_width)
    row_ids = row_offset + jnp.arange(row_width, dtype=jnp.int32)
    col_ids = col_offset + jnp.arange(col_width, dtype=jnp.int32)
    first_column = lax.axis_index(COL) == 0
    identity = jnp.eye(PANEL, dtype=jnp.float32)
    for panel_index in range(PANELS):
        start = panel_index * PANEL
        finish = start + PANEL
        rows_now = from_root(front[start:finish, :].astype(jnp.bfloat16), "row", 0).astype(
            jnp.float32
        )
        pivot = jnp.where(first_column, rows_now[:, start:finish], identity)
        inverse = invert(pivot)
        below = (row_ids >= finish)[:, None]
        lower = jnp.where(
            below, jnp.dot(front[:, start:finish], inverse, precision=lax.Precision.HIGHEST), 0.0
        )
        lower_b = broadcast_by_axis(lower.astype(jnp.bfloat16), COL, 0)
        upper_b = jnp.where((col_ids >= finish)[None, :], rows_now, 0.0).astype(jnp.bfloat16)
        front = front - jnp.dot(lower_b, upper_b, preferred_element_type=jnp.float32)
        front = front.at[:, start:finish].set(
            jnp.where(below & first_column, lower, front[:, start:finish])
        )
    return front[None]


def solution(mesh):
    finer = Mesh(
        mesh.devices.reshape(mesh.shape["front"], mesh.shape["row"], 4, 2),
        ("front", "row", "col_0", "col_1"),
    )
    in_specs = (
        P("front", "row", COL),
        P("front", ROW_COL, None),
        P("front", ROW_COL, None),
        P("front", ROW_COL, None),
        P(),
        P(),
    )
    out_specs = P("front", "row", COL)
    return jax.shard_map(local, mesh=finer, in_specs=in_specs, out_specs=out_specs, check_vma=False)
```

profile of v0, /device:TPU:1, one launch (start us, length us, event | category | flops | bytes accessed | tf_op | source)
XLA Modules:
  0.0 1218.4 jit_solution(10147357242169241187)
XLA Ops:
  18.6 157.3 %all-gather.10.cloned.1.call-done = bf16[4,4096,512]{2,1,0:T(8,128)(2,1)} async-done(((bf16[4,128,512]{2,1,0:T(8,128)(2,1)}), bf16[4,4096,512]{2,1,0:T(8,128)(2,1)}) %all-gather.10.cloned.1.call-update) | async-done | bytes 16777232 | tf_op jit(solution)/shard_map/all_gather | solution.py:117
  183.2 81.0 %scatter_custom_fusion = f32[2048,256]{1,0:T(8,128)S(1)} fusion(s32[16384]{0:T(1024)S(1)} %bitcast.206, bf16[16384,256]{1,0:T(8,128)(2,1)} %bitcast.198, f32[]{:T(128)} %constant.285.clone.1), kind=kCustom, calls=%fused_computation.11 | custom fusion | flops 8388608 | bytes 10485764 | tf_op jit(solution)/shard_map/scatter-add | solution.py:60
  283.6 43.2 %scatter_custom_fusion.1 = bf16[8192,128]{1,0:T(8,128)(2,1)} fusion(s32[16384]{0:T(1024)S(1)} %bitcast.208, bf16[16384,128]{1,0:T(8,128)(2,1)} %bitcast.204, bf16[]{:T(256)} %constant.269.clone.1), kind=kCustom, calls=%fused_computation.55 | custom fusion | bytes 2097664
  328.5 41.6 %scatter_custom_fusion.2 = bf16[4096,128]{1,0:T(8,128)(2,1)S(1)} fusion(s32[16384]{0:T(1024)S(1)} %bitcast.207, bf16[16384,128]{1,0:T(8,128)(2,1)} %bitcast.203, bf16[]{:T(256)} %constant.269.clone.1), kind=kCustom, calls=%fused_computation.77 | custom fusion | bytes 1049088
  383.1 29.5 %all-gather.12.cloned.1.call-done = bf16[1024,1024]{1,0:T(8,128)(2,1)} async-done(((bf16[256,1024]{1,0:T(8,128)(2,1)}), bf16[1024,1024]{1,0:T(8,128)(2,1)}) %all-gather.12.cloned.1.call-update) | async-done | bytes 2097168 | tf_op jit(solution)/shard_map/all_gather | solution.py:19
  436.6 11.7 cholesky.231
  455.4 19.7 %custom-call.20 = f32[2,128,128]{1,2,0:T(8,128)S(1)} custom-call(f32[2,128,128]{2,1,0:T(8,128)S(1)} %get-tuple-element.81), custom_call_target="InvertDiagBlocksLowerTriangular" | custom-call | tf_op jit(solution)/shard_map/jit(_cho_solve)/triangular_solve | solution.py:32
  481.5 44.4 %all-reduce.10.cloned.1.call-done = bf16[2048,256]{1,0:T(8,128)(2,1)} async-done(((bf16[2048,256]{1,0:T(8,128)(2,1)}), bf16[2048,256]{1,0:T(8,128)(2,1)}) %all-reduce.10.cloned.1.call-update) | async-done | bytes 1048592 | tf_op jit(solution)/shard_map/psum | solution.py:25
  526.6 52.4 %all-reduce.12.cloned.1.call-done = bf16[2048,256]{1,0:T(8,128)(2,1)} async-done(((bf16[2048,256]{1,0:T(8,128)(2,1)}), bf16[2048,256]{1,0:T(8,128)(2,1)}) %all-reduce.12.cloned.1.call-update) | async-done | bytes 1048592 | tf_op jit(solution)/shard_map/psum | solution.py:25
  589.9 30.4 %all-gather.14.cloned.1.call-done = bf16[1024,1024]{1,0:T(8,128)(2,1)} async-done(((bf16[256,1024]{1,0:T(8,128)(2,1)}), bf16[1024,1024]{1,0:T(8,128)(2,1)}) %all-gather.14.cloned.1.call-update) | async-done | bytes 2097168 | tf_op jit(solution)/shard_map/all_gather | solution.py:19
  644.3 11.7 cholesky.265
  662.7 19.7 %custom-call.22 = f32[2,128,128]{1,2,0:T(8,128)S(1)} custom-call(f32[2,128,128]{2,1,0:T(8,128)S(1)} %get-tuple-element.82), custom_call_target="InvertDiagBlocksLowerTriangular" | custom-call | tf_op jit(solution)/shard_map/jit(_cho_solve)/triangular_solve | solution.py:32
  688.8 44.3 %all-reduce.14.cloned.1.call-done = bf16[2048,256]{1,0:T(8,128)(2,1)} async-done(((bf16[2048,256]{1,0:T(8,128)(2,1)}), bf16[2048,256]{1,0:T(8,128)(2,1)}) %all-reduce.14.cloned.1.call-update) | async-done | bytes 1048592 | tf_op jit(solution)/shard_map/psum | solution.py:25
  733.9 52.5 %all-reduce.16.cloned.1.call-done = bf16[2048,256]{1,0:T(8,128)(2,1)} async-done(((bf16[2048,256]{1,0:T(8,128)(2,1)}), bf16[2048,256]{1,0:T(8,128)(2,1)}) %all-reduce.16.cloned.1.call-update) | async-done | bytes 1048592 | tf_op jit(solution)/shard_map/psum | solution.py:25
  797.5 30.1 %all-gather.16.cloned.1.call-done = bf16[1024,1024]{1,0:T(8,128)(2,1)} async-done(((bf16[256,1024]{1,0:T(8,128)(2,1)}), bf16[1024,1024]{1,0:T(8,128)(2,1)}) %all-gather.16.cloned.1.call-update) | async-done | bytes 2097168 | tf_op jit(solution)/shard_map/all_gather | solution.py:19
  851.7 11.7 cholesky.299
  870.1 19.7 %custom-call.24 = f32[2,128,128]{1,2,0:T(8,128)S(1)} custom-call(f32[2,128,128]{2,1,0:T(8,128)S(1)} %get-tuple-element.83), custom_call_target="InvertDiagBlocksLowerTriangular" | custom-call | tf_op jit(solution)/shard_map/jit(_cho_solve)/triangular_solve | solution.py:32
  896.3 44.4 %all-reduce.18.cloned.1.call-done = bf16[2048,256]{1,0:T(8,128)(2,1)} async-done(((bf16[2048,256]{1,0:T(8,128)(2,1)}), bf16[2048,256]{1,0:T(8,128)(2,1)}) %all-reduce.18.cloned.1.call-update) | async-done | bytes 1048592 | tf_op jit(solution)/shard_map/psum | solution.py:25
  941.4 52.3 %all-reduce.20.cloned.1.call-done = bf16[2048,256]{1,0:T(8,128)(2,1)} async-done(((bf16[2048,256]{1,0:T(8,128)(2,1)}), bf16[2048,256]{1,0:T(8,128)(2,1)}) %all-reduce.20.cloned.1.call-update) | async-done | bytes 1048592 | tf_op jit(solution)/shard_map/psum | solution.py:25
  1004.7 30.3 %all-gather.18.cloned.1.call-done = bf16[1024,1024]{1,0:T(8,128)(2,1)} async-done(((bf16[256,1024]{1,0:T(8,128)(2,1)}), bf16[1024,1024]{1,0:T(8,128)(2,1)}) %all-gather.18.cloned.1.call-update) | async-done | bytes 2097168 | tf_op jit(solution)/shard_map/all_gather | solution.py:19
  1059.1 11.7 cholesky.333
  1077.6 19.7 %custom-call.26 = f32[2,128,128]{1,2,0:T(8,128)S(1)} custom-call(f32[2,128,128]{2,1,0:T(8,128)S(1)} %get-tuple-element.84), custom_call_target="InvertDiagBlocksLowerTriangular" | custom-call | tf_op jit(solution)/shard_map/jit(_cho_solve)/triangular_solve | solution.py:32
  1103.7 44.4 %all-reduce.22.cloned.1.call-done = bf16[2048,256]{1,0:T(8,128)(2,1)} async-done(((bf16[2048,256]{1,0:T(8,128)(2,1)}), bf16[2048,256]{1,0:T(8,128)(2,1)}) %all-reduce.22.cloned.1.call-update) | async-done | bytes 1048592 | tf_op jit(solution)/shard_map/psum | solution.py:25
  1148.1 53.2 %all-reduce.24.cloned.1.call-done = bf16[2048,256]{1,0:T(8,128)(2,1)} async-done(((bf16[2048,256]{1,0:T(8,128)(2,1)}), bf16[2048,256]{1,0:T(8,128)(2,1)}) %all-reduce.24.cloned.1.call-update) | async-done | bytes 1048592 | tf_op jit(solution)/shard_map/psum | solution.py:25
  (230 shorter events, 257.3 us)
Async XLA Ops:
  6.5 10.9 copy-start
  6.5 11.3 copy-start.9
  6.5 11.5 copy-start.7
  6.5 11.5 copy-start.8
  6.5 11.8 copy-start.10
  6.5 169.3 %all-gather.10.cloned.1.call-start = ((), (), s32[]{:S(2)}) async-start(), calls=%async_computation | async-start | bytes 17301504 | tf_op jit(solution)/shard_map/all_gather | solution.py:117
  7.7 8.8 collective-permute-start
  17.3 395.3 %all-gather.12.cloned.1.call-start = ((), (), s32[]{:S(2)}) async-start(), calls=%async_computation.9 | async-start | bytes 2621440 | tf_op jit(solution)/shard_map/all_gather | solution.py:19
  378.7 3.4 copy-start.5
  383.0 142.9 %all-reduce.10.cloned.1.call-start = ((), (), s32[]{:S(2)}) async-start(), calls=%async_computation.1 | async-start | bytes 2097152 | tf_op jit(solution)/shard_map/psum | solution.py:25
  481.4 97.5 %all-reduce.12.cloned.1.call-start = ((), (), s32[]{:S(2)}) async-start(), calls=%async_computation.2 | async-start | bytes 2097152 | tf_op jit(solution)/shard_map/psum | solution.py:25
  525.8 94.4 %all-gather.14.cloned.1.call-start = ((), (), s32[]{:S(2)}) async-start(), calls=%async_computation.10 | async-start | bytes 2621440 | tf_op jit(solution)/shard_map/all_gather | solution.py:19
  585.3 3.4 copy-start.2
  589.6 143.5 %all-reduce.14.cloned.1.call-start = ((), (), s32[]{:S(2)}) async-start(), calls=%async_computation.3 | async-start | bytes 2097152 | tf_op jit(solution)/shard_map/psum | solution.py:25
  688.8 97.6 %all-reduce.16.cloned.1.call-start = ((), (), s32[]{:S(2)}) async-start(), calls=%async_computation.4 | async-start | bytes 2097152 | tf_op jit(solution)/shard_map/psum | solution.py:25
  733.1 94.5 %all-gather.16.cloned.1.call-start = ((), (), s32[]{:S(2)}) async-start(), calls=%async_computation.11 | async-start | bytes 2621440 | tf_op jit(solution)/shard_map/all_gather | solution.py:19
  792.8 3.4 copy-start.3
  797.1 143.6 %all-reduce.18.cloned.1.call-start = ((), (), s32[]{:S(2)}) async-start(), calls=%async_computation.5 | async-start | bytes 2097152 | tf_op jit(solution)/shard_map/psum | solution.py:25
  896.2 97.5 %all-reduce.20.cloned.1.call-start = ((), (), s32[]{:S(2)}) async-start(), calls=%async_computation.6 | async-start | bytes 2097152 | tf_op jit(solution)/shard_map/psum | solution.py:25
  940.7 94.4 %all-gather.18.cloned.1.call-start = ((), (), s32[]{:S(2)}) async-start(), calls=%async_computation.12 | async-start | bytes 2621440 | tf_op jit(solution)/shard_map/all_gather | solution.py:19
  1000.2 3.4 copy-start.4
  1004.5 143.6 %all-reduce.22.cloned.1.call-start = ((), (), s32[]{:S(2)}) async-start(), calls=%async_computation.7 | async-start | bytes 2097152 | tf_op jit(solution)/shard_map/psum | solution.py:25
  1103.7 97.6 %all-reduce.24.cloned.1.call-start = ((), (), s32[]{:S(2)}) async-start(), calls=%async_computation.8 | async-start | bytes 2097152 | tf_op jit(solution)/shard_map/psum | solution.py:25
  1209.9 1.6 copy-start.1
  (1 other events, 0.8 us)
Sparse Core Ops, SparseCore 0:
  17.4 158.3 all-gather.9
  383.1 29.4 all-gather.11
  481.5 44.2 all-reduce.9
  528.1 50.7 all-reduce.11
  589.7 30.4 all-gather.13
  688.9 44.1 all-reduce.13
  735.6 50.7 all-reduce.15
  797.2 30.4 all-gather.15
  896.3 44.2 all-reduce.17
  943.0 50.7 all-reduce.19
  1004.6 30.4 all-gather.17
  1103.8 44.2 all-reduce.21
  1150.5 50.7 all-reduce.23
where the time goes:
time: 1230 us; the launch traced here: 1220 us
  waiting for transfers between devices  672 us (55%)
  other arithmetic  319 us (26%)
  local copies, waits for them, and re-layouts  144 us (12%)
  matrix products  58.6 us (5%)
  between operations  19.6 us (2%)
    psum x8, waiting for transfers between devices, broadcast_by_axis(): value = lax.psum(value, axis)  388 us
    all_gather x1, waiting for transfers between devices, local(): lax.all_gather(moved, ROW_COL, axis=1, tiled=True)  157 us
    another operation x28, other arithmetic, invert(): factor = jnp.linalg.cholesky(gram)  138 us
    all_gather x4, waiting for transfers between devices, from_root(): lax.all_gather(value, axis)  120 us
    unnamed x30, local copies, waits for them, and re-layouts  111 us
    scatter-add x1, other arithmetic, place_rows(): rows_d.at[local_row]  81 us
    another operation x9, other arithmetic, invert(): return jax.scipy.linalg.cho_solve((factor, True), block.T)  78.8 us
  transfers between devices with their start and end apart: 14, of which 14 were waited for; matrix products, arithmetic and copies ran while one was open for 0% of the time, Pallas kernels for 0%

commit v1 on v0

--- a/solution.py
+++ b/solution.py
@@ -114,7 +114,11 @@
         blocks, row_offset, col_offset, row_width, col_width, rank_width, leaf_width
     )
     collected = place_rows(
-        empty_carry, lax.all_gather(moved, ROW_COL, axis=1, tiled=True), jnp.int32(0)
+        empty_carry,
+        jnp.concatenate(
+            lax.all_to_all(jnp.stack([moved] * lax.axis_size(ROW_COL)), ROW_COL, 0, 0), axis=1
+        ),
+        jnp.int32(0),
     )
     front = front_entries[0] + expand_tile(collected, counts, row_offset, col_offset, leaf_width)
     row_ids = row_offset + jnp.arange(row_width, dtype=jnp.int32)

time: 1230 us -> 1370 us (1.11)
  waiting for transfers between devices: 672 us -> 788 us
  local copies, waits for them, and re-layouts: 144 us -> 163 us
    all_to_all x0 -> x1, waiting for transfers between devices: none -> 251 us  [local(): lax.all_to_all(jnp.stack([moved] * lax.axis_size(ROW_COL)), ROW_COL, 0, 0)]
    all_gather x1 -> x0, waiting for transfers between devices: 157 us -> none  [local(): lax.all_gather(moved, ROW_COL, axis=1, tiled=True)]
    all_gather x4, waiting for transfers between devices: 120 us -> 142 us  [from_root(): lax.all_gather(value, axis)]
    all_to_all x0 -> x1, local copies, waits for them, and re-layouts: none -> 13.9 us  [local(): lax.all_to_all(jnp.stack([moved] * lax.axis_size(ROW_COL)), ROW_COL, 0, 0)]
    unnamed x30 -> x28, local copies, waits for them, and re-layouts: 111 us -> 110 us
where the time goes in v1:
time: 1370 us; the launch traced here: 1360 us
  waiting for transfers between devices  788 us (58%)
  other arithmetic  319 us (23%)
  local copies, waits for them, and re-layouts  163 us (12%)
  matrix products  58.6 us (4%)
  between operations  19.9 us (1%)
  starting transfers between devices  14.4 us (1%)
    psum x8, waiting for transfers between devices, broadcast_by_axis(): value = lax.psum(value, axis)  388 us
    all_to_all x1, waiting for transfers between devices, local(): lax.all_to_all(jnp.stack([moved] * lax.axis_size(ROW_COL)), ROW_COL, 0, 0)  251 us
    all_gather x4, waiting for transfers between devices, from_root(): lax.all_gather(value, axis)  142 us
    another operation x28, other arithmetic, invert(): factor = jnp.linalg.cholesky(gram)  138 us
    unnamed x28, local copies, waits for them, and re-layouts  110 us
    scatter-add x1, other arithmetic, place_rows(): rows_d.at[local_row]  81 us
    another operation x9, other arithmetic, invert(): return jax.scipy.linalg.cho_solve((factor, True), block.T)  78.8 us
  transfers between devices with their start and end apart: 14, of which 14 were waited for; matrix products, arithmetic and copies ran while one was open for 0% of the time, Pallas kernels for 0%

profile of v1, /device:TPU:1, one launch (start us, length us, event | category | flops | bytes accessed | tf_op | source)
XLA Modules:
  0.0 1364.2 jit_solution(3054898354999483302)
XLA Ops:
  34.1 251.5 %all-to-all-done = bf16[32,4,128,512]{3,2,1,0:T(8,128)(2,1)} async-done(((bf16[32,4,128,512]{3,2,1,0:T(8,128)(2,1)}), bf16[32,4,128,512]{3,2,1,0:T(8,128)(2,1)}, u32[]{:S(2)}, u32[]{:S(2)}) %all-to-all-start) | async-done | bytes 16777248 | tf_op jit(solution)/shard_map/all_to_all | solution.py:119
  285.6 13.9 %copy.38 = bf16[32,4,128,512]{3,2,0,1:T(8,128)(2,1)} copy(bf16[32,4,128,512]{3,2,1,0:T(8,128)(2,1)} %all-to-all-done) | data formatting | bytes 33554432 | tf_op jit(solution)/shard_map/all_to_all | solution.py:119
  312.6 81.0 %scatter_custom_fusion = f32[2048,256]{1,0:T(8,128)S(1)} fusion(s32[16384]{0:T(1024)S(1)} %bitcast.211, bf16[16384,256]{1,0:T(8,128)(2,1)} %bitcast.202, f32[]{:T(128)} %constant.285.clone.1), kind=kCustom, calls=%fused_computation.11 | custom fusion | flops 8388608 | bytes 10485764 | tf_op jit(solution)/shard_map/scatter-add | solution.py:60
  407.3 43.1 %scatter_custom_fusion.1 = bf16[8192,128]{1,0:T(8,128)(2,1)} fusion(s32[16384]{0:T(1024)S(1)} %bitcast.213, bf16[16384,128]{1,0:T(8,128)(2,1)} %bitcast.209, bf16[]{:T(256)} %constant.269.clone.1), kind=kCustom, calls=%fused_computation.55 | custom fusion | bytes 2097664
  452.2 41.6 %scatter_custom_fusion.2 = bf16[4096,128]{1,0:T(8,128)(2,1)S(1)} fusion(s32[16384]{0:T(1024)S(1)} %bitcast.212, bf16[16384,128]{1,0:T(8,128)(2,1)} %bitcast.208, bf16[]{:T(256)} %constant.269.clone.1), kind=kCustom, calls=%fused_computation.77 | custom fusion | bytes 1049088
  506.7 51.4 %all-gather.9.cloned.1.call-done = bf16[1024,1024]{1,0:T(8,128)(2,1)} async-done(((bf16[256,1024]{1,0:T(8,128)(2,1)}), bf16[1024,1024]{1,0:T(8,128)(2,1)}) %all-gather.9.cloned.1.call-update) | async-done | bytes 2097168 | tf_op jit(solution)/shard_map/all_gather | solution.py:19
  582.2 11.7 cholesky.231
  600.9 19.7 %custom-call.20 = f32[2,128,128]{1,2,0:T(8,128)S(1)} custom-call(f32[2,128,128]{2,1,0:T(8,128)S(1)} %get-tuple-element.81), custom_call_target="InvertDiagBlocksLowerTriangular" | custom-call | tf_op jit(solution)/shard_map/jit(_cho_solve)/triangular_solve | solution.py:32
  627.0 44.3 %all-reduce.10.cloned.1.call-done = bf16[2048,256]{1,0:T(8,128)(2,1)} async-done(((bf16[2048,256]{1,0:T(8,128)(2,1)}), bf16[2048,256]{1,0:T(8,128)(2,1)}) %all-reduce.10.cloned.1.call-update) | async-done | bytes 1048592 | tf_op jit(solution)/shard_map/psum | solution.py:25
  672.0 52.5 %all-reduce.12.cloned.1.call-done = bf16[2048,256]{1,0:T(8,128)(2,1)} async-done(((bf16[2048,256]{1,0:T(8,128)(2,1)}), bf16[2048,256]{1,0:T(8,128)(2,1)}) %all-reduce.12.cloned.1.call-update) | async-done | bytes 1048592 | tf_op jit(solution)/shard_map/psum | solution.py:25
  735.5 30.4 %all-gather.11.cloned.1.call-done = bf16[1024,1024]{1,0:T(8,128)(2,1)} async-done(((bf16[256,1024]{1,0:T(8,128)(2,1)}), bf16[1024,1024]{1,0:T(8,128)(2,1)}) %all-gather.11.cloned.1.call-update) | async-done | bytes 2097168 | tf_op jit(solution)/shard_map/all_gather | solution.py:19
  808.3 19.7 %custom-call.22 = f32[2,128,128]{1,2,0:T(8,128)S(1)} custom-call(f32[2,128,128]{2,1,0:T(8,128)S(1)} %get-tuple-element.82), custom_call_target="InvertDiagBlocksLowerTriangular" | custom-call | tf_op jit(solution)/shard_map/jit(_cho_solve)/triangular_solve | solution.py:32
  834.5 44.3 %all-reduce.14.cloned.1.call-done = bf16[2048,256]{1,0:T(8,128)(2,1)} async-done(((bf16[2048,256]{1,0:T(8,128)(2,1)}), bf16[2048,256]{1,0:T(8,128)(2,1)}) %all-reduce.14.cloned.1.call-update) | async-done | bytes 1048592 | tf_op jit(solution)/shard_map/psum | solution.py:25
  879.5 52.4 %all-reduce.16.cloned.1.call-done = bf16[2048,256]{1,0:T(8,128)(2,1)} async-done(((bf16[2048,256]{1,0:T(8,128)(2,1)}), bf16[2048,256]{1,0:T(8,128)(2,1)}) %all-reduce.16.cloned.1.call-update) | async-done | bytes 1048592 | tf_op jit(solution)/shard_map/psum | solution.py:25
  943.0 30.1 %all-gather.13.cloned.1.call-done = bf16[1024,1024]{1,0:T(8,128)(2,1)} async-done(((bf16[256,1024]{1,0:T(8,128)(2,1)}), bf16[1024,1024]{1,0:T(8,128)(2,1)}) %all-gather.13.cloned.1.call-update) | async-done | bytes 2097168 | tf_op jit(solution)/shard_map/all_gather | solution.py:19
  997.2 11.7 cholesky.299
  1015.6 19.7 %custom-call.24 = f32[2,128,128]{1,2,0:T(8,128)S(1)} custom-call(f32[2,128,128]{2,1,0:T(8,128)S(1)} %get-tuple-element.83), custom_call_target="InvertDiagBlocksLowerTriangular" | custom-call | tf_op jit(solution)/shard_map/jit(_cho_solve)/triangular_solve | solution.py:32
  1041.7 44.4 %all-reduce.18.cloned.1.call-done = bf16[2048,256]{1,0:T(8,128)(2,1)} async-done(((bf16[2048,256]{1,0:T(8,128)(2,1)}), bf16[2048,256]{1,0:T(8,128)(2,1)}) %all-reduce.18.cloned.1.call-update) | async-done | bytes 1048592 | tf_op jit(solution)/shard_map/psum | solution.py:25
  1086.9 52.5 %all-reduce.20.cloned.1.call-done = bf16[2048,256]{1,0:T(8,128)(2,1)} async-done(((bf16[2048,256]{1,0:T(8,128)(2,1)}), bf16[2048,256]{1,0:T(8,128)(2,1)}) %all-reduce.20.cloned.1.call-update) | async-done | bytes 1048592 | tf_op jit(solution)/shard_map/psum | solution.py:25
  1150.4 30.3 %all-gather.15.cloned.1.call-done = bf16[1024,1024]{1,0:T(8,128)(2,1)} async-done(((bf16[256,1024]{1,0:T(8,128)(2,1)}), bf16[1024,1024]{1,0:T(8,128)(2,1)}) %all-gather.15.cloned.1.call-update) | async-done | bytes 2097168 | tf_op jit(solution)/shard_map/all_gather | solution.py:19
  1204.8 11.7 cholesky.333
  1223.3 19.7 %custom-call.26 = f32[2,128,128]{1,2,0:T(8,128)S(1)} custom-call(f32[2,128,128]{2,1,0:T(8,128)S(1)} %get-tuple-element.84), custom_call_target="InvertDiagBlocksLowerTriangular" | custom-call | tf_op jit(solution)/shard_map/jit(_cho_solve)/triangular_solve | solution.py:32
  1249.4 44.4 %all-reduce.22.cloned.1.call-done = bf16[2048,256]{1,0:T(8,128)(2,1)} async-done(((bf16[2048,256]{1,0:T(8,128)(2,1)}), bf16[2048,256]{1,0:T(8,128)(2,1)}) %all-reduce.22.cloned.1.call-update) | async-done | bytes 1048592 | tf_op jit(solution)/shard_map/psum | solution.py:25
  1293.8 53.0 %all-reduce.24.cloned.1.call-done = bf16[2048,256]{1,0:T(8,128)(2,1)} async-done(((bf16[2048,256]{1,0:T(8,128)(2,1)}), bf16[2048,256]{1,0:T(8,128)(2,1)}) %all-reduce.24.cloned.1.call-update) | async-done | bytes 1048592 | tf_op jit(solution)/shard_map/psum | solution.py:25
  (229 shorter events, 284.5 us)
Async XLA Ops:
  6.5 26.4 %copy-start = (s32[16,16]{1,0:T(8,128)S(1)}, s32[16,16]{1,0:T(8,128)}, u32[]{:S(2)}) copy-start(s32[16,16]{1,0:T(8,128)} %param.22) | copy-start | bytes 3076
  7.6 8.8 collective-permute-start
  22.4 11.1 copy-start.8
  22.4 11.2 copy-start.6
  22.4 11.2 copy-start.7
  22.4 263.2 %all-to-all-start = ((bf16[32,4,128,512]{3,2,1,0:T(8,128)(2,1)}), bf16[32,4,128,512]{3,2,1,0:T(8,128)(2,1)}, u32[]{:S(2)}, u32[]{:S(2)}) async-start(bf16[32,4,128,512]{3,2,1,0:T(8,128)(2,1)} %stack.2), calls=%async_computation | async-start | bytes 33554432 | tf_op jit(solution)/shard_map/all_to_all | solution.py:119
  32.9 1.0 copy-start.9
  32.9 525.2 %all-gather.9.cloned.1.call-start = ((), (), s32[]{:S(2)}) async-start(), calls=%async_computation.9 | async-start | bytes 2621440 | tf_op jit(solution)/shard_map/all_gather | solution.py:19
  502.3 3.4 copy-start.5
  506.6 164.7 %all-reduce.10.cloned.1.call-start = ((), (), s32[]{:S(2)}) async-start(), calls=%async_computation.1 | async-start | bytes 2097152 | tf_op jit(solution)/shard_map/psum | solution.py:25
  626.9 97.6 %all-reduce.12.cloned.1.call-start = ((), (), s32[]{:S(2)}) async-start(), calls=%async_computation.2 | async-start | bytes 2097152 | tf_op jit(solution)/shard_map/psum | solution.py:25
  671.3 94.5 %all-gather.11.cloned.1.call-start = ((), (), s32[]{:S(2)}) async-start(), calls=%async_computation.10 | async-start | bytes 2621440 | tf_op jit(solution)/shard_map/all_gather | solution.py:19
  730.9 3.4 copy-start.2
  735.2 143.5 %all-reduce.14.cloned.1.call-start = ((), (), s32[]{:S(2)}) async-start(), calls=%async_computation.3 | async-start | bytes 2097152 | tf_op jit(solution)/shard_map/psum | solution.py:25
  834.4 97.4 %all-reduce.16.cloned.1.call-start = ((), (), s32[]{:S(2)}) async-start(), calls=%async_computation.4 | async-start | bytes 2097152 | tf_op jit(solution)/shard_map/psum | solution.py:25
  878.8 94.4 %all-gather.13.cloned.1.call-start = ((), (), s32[]{:S(2)}) async-start(), calls=%async_computation.11 | async-start | bytes 2621440 | tf_op jit(solution)/shard_map/all_gather | solution.py:19
  938.3 3.4 copy-start.3
  942.6 143.6 %all-reduce.18.cloned.1.call-start = ((), (), s32[]{:S(2)}) async-start(), calls=%async_computation.5 | async-start | bytes 2097152 | tf_op jit(solution)/shard_map/psum | solution.py:25
  1041.7 97.7 %all-reduce.20.cloned.1.call-start = ((), (), s32[]{:S(2)}) async-start(), calls=%async_computation.6 | async-start | bytes 2097152 | tf_op jit(solution)/shard_map/psum | solution.py:25
  1086.2 94.5 %all-gather.15.cloned.1.call-start = ((), (), s32[]{:S(2)}) async-start(), calls=%async_computation.12 | async-start | bytes 2621440 | tf_op jit(solution)/shard_map/all_gather | solution.py:19
  1145.8 3.4 copy-start.4
  1150.1 143.6 %all-reduce.22.cloned.1.call-start = ((), (), s32[]{:S(2)}) async-start(), calls=%async_computation.7 | async-start | bytes 2097152 | tf_op jit(solution)/shard_map/psum | solution.py:25
  1249.3 97.5 %all-reduce.24.cloned.1.call-start = ((), (), s32[]{:S(2)}) async-start(), calls=%async_computation.8 | async-start | bytes 2097152 | tf_op jit(solution)/shard_map/psum | solution.py:25
  1355.4 1.6 copy-start.1
Sparse Core Ops, SparseCore 0:
  506.7 51.3 all-gather.8
  627.0 44.2 all-reduce.9
  673.8 50.7 all-reduce.11
  735.4 30.4 all-gather.10
  834.5 44.1 all-reduce.13
  881.1 50.7 all-reduce.15
  942.7 30.4 all-gather.12
  1041.8 44.3 all-reduce.17
  1088.6 50.7 all-reduce.19
  1150.3 30.4 all-gather.14
  1249.5 44.2 all-reduce.21
  1296.1 50.7 all-reduce.23
